TPU v7x, 32 devices: a whole 2x2x4 slice. The times are simulated.
32 devices in a mesh: dp: 4 (over y, x), expert: 8 (over z, core).
Axes of the slice: x: 2, y: 2, z: 4, core: 2. Of those that a mesh axis runs over, the one named last changes fastest.
Arguments:
- hidden: bfloat16 [8, 4608, 1408], P('expert', 'dp')
- upstream: bfloat16 [8, 4608, 2048], P('expert', 'dp')
- token_counts: int32 [8, 4], P('expert', 'dp'), may hold values from 1 to 1152, as said below
- master: float32 [8, 1408, 2048], P('expert', 'dp'), may hold values from -0.15625 to 0.15625
- first_moment: float32 [8, 1408, 2048], P('expert', 'dp'), may hold values from -6 to 6
- second_moment: float32 [8, 1408, 2048], P('expert', 'dp'), may hold values from 0.25 to 4
- router_input: bfloat16 [4096, 2048], P(('dp', 'expert')), may hold values from -6 to 6
- router_cot: bfloat16 [64, 4096], P(None, ('dp', 'expert'))
- router_master: float32 [64, 2048], replicated, may hold values from -0.125 to 0.125
- router_first: float32 [64, 2048], replicated, may hold values from -6 to 6
- router_second: float32 [64, 2048], replicated, may hold values from 0.25 to 4
- partner: int32 [8], replicated, may hold values from 0 to 7, as said below
Outputs:
- new_weight: bfloat16 [8, 1408, 2048], P('expert')
- new_master: float32 [8, 1408, 2048], P('expert', 'dp')
- new_first: float32 [8, 1408, 2048], P('expert', 'dp')
- new_second: float32 [8, 1408, 2048], P('expert', 'dp')
- router_master_new: float32 [64, 2048], replicated
- router_first_new: float32 [64, 2048], replicated
- router_second_new: float32 [64, 2048], replicated
Inputs may be any that keep to these rules, and one draw needn't show every extreme that they name: partner[partner[p]] = p for every position p; a position with partner[p] = p keeps its expert. The first token_counts[e, d] of replica d's 1152 slots for position e are live, the rest are padding.
All inputs are finite; a program needn't handle non-finite values.
Results may differ from a plain program's by a relative error of at most 0.001.
Values may be sent and summed in bfloat16 or wider, within the bound.
A program may use at most 128 MiB of HBM per device.

v0:
```python
import math
import jax
import jax.numpy as jnp
from jax import lax
from jax.sharding import PartitionSpec as P

beta_first = 0.9
beta_second = 0.95
learn_rate = 0.001
decay_weight = 0.1
adam_eps = 1e-08
norm_eps = 1e-06
correct_first = 1.0 - 0.9**10
correct_second = 1.0 - 0.95**10


def adam_update(gradient, moment_one, moment_two, weights):
    first_new = beta_first * moment_one + (1.0 - beta_first) * gradient
    second_new = beta_second * moment_two + (1.0 - beta_second) * gradient * gradient
    ratio = first_new / correct_first / (jnp.sqrt(second_new / correct_second) + adam_eps)
    weights_new = weights - learn_rate * (ratio + decay_weight * weights)
    return (weights_new, first_new, second_new)


def split_pieces(matrix, groups):
    return matrix.reshape(matrix.shape[0], groups, matrix.shape[1] // groups)


def relocate_state(states, partner):
    groups = lax.axis_size("expert")
    pieces = tuple((split_pieces(member, groups) for member in states))

    def reorder(received):
        arranged = tuple((jnp.take(member, partner, axis=1) for member in received))
        return lax.all_to_all(arranged, "expert", split_axis=1, concat_axis=1, tiled=True)

    result = reorder(
        (
            lax.all_to_all(pieces[0], "expert", split_axis=1, concat_axis=1, tiled=True),
            lax.all_to_all(pieces[1], "expert", split_axis=1, concat_axis=1, tiled=True),
            lax.all_to_all(pieces[2], "expert", split_axis=1, concat_axis=1, tiled=True),
        )
    )
    return tuple((member.reshape(member.shape[0], -1) for member in result))


def regather(weight_shard):
    return lax.all_gather(weight_shard, "dp", axis=0, tiled=True)


def on_device(
    hidden,
    upstream,
    token_counts,
    master,
    first_moment,
    second_moment,
    router_input,
    router_cot,
    router_master,
    router_first,
    router_second,
    partner,
):
    hidden_units = hidden.shape[2]
    features = upstream.shape[2]
    row_count = hidden.shape[1]
    live_rows = jnp.arange(row_count, dtype=jnp.int32) < token_counts[0, 0]
    activations = hidden[0]
    grads_out = upstream[0]
    masked_out = jnp.where(live_rows[:, None], grads_out, jnp.zeros_like(grads_out))
    router_partial = jnp.dot(router_cot, router_input, preferred_element_type=jnp.float32)
    gradient = lax.psum_scatter(
        lax.dot_general(
            activations, masked_out, (((0,), (0,)), ((), ())), preferred_element_type=jnp.float32
        ),
        "dp",
        scatter_dimension=0,
        tiled=True,
    )
    router_grad, expert_square = lax.psum(
        (router_partial, jnp.sum(gradient * gradient)), ("dp", "expert")
    )
    total_square = expert_square + jnp.sum(router_grad * router_grad)
    clip_limit = 2.0 * math.sqrt(
        float(lax.axis_size("expert") * hidden_units * features + router_cot.shape[0] * features)
    )
    factor = jnp.minimum(1.0, clip_limit / (jnp.sqrt(total_square) + norm_eps))
    master_new, first_new, second_new = adam_update(
        factor * gradient, first_moment[0], second_moment[0], master[0]
    )
    router_outs = adam_update(factor * router_grad, router_first, router_second, router_master)
    moved = relocate_state((master_new, first_new, second_new), partner)
    moved_weight = regather(moved[0].astype(jnp.bfloat16))
    return (
        moved_weight[None],
        moved[0][None],
        moved[1][None],
        moved[2][None],
        router_outs[0],
        router_outs[1],
        router_outs[2],
    )


def solution(mesh):
    in_specs = (
        P("expert", "dp", None),
        P("expert", "dp", None),
        P("expert", "dp"),
        P("expert", "dp", None),
        P("expert", "dp", None),
        P("expert", "dp", None),
        P(("dp", "expert"), None),
        P(None, ("dp", "expert")),
        P(),
        P(),
        P(),
        P(),
    )
    out_specs = (
        P("expert", None, None),
        P("expert", "dp", None),
        P("expert", "dp", None),
        P("expert", "dp", None),
        P(),
        P(),
        P(),
    )
    return jax.shard_map(
        on_device, mesh=mesh, in_specs=in_specs, out_specs=out_specs, check_vma=False
    )
```

profile of v0, /device:TPU:0, one launch (start us, length us, event | category | flops | bytes accessed | tf_op | source)
XLA Modules:
  0.0 716.0 jit_solution(1665810783923439618)
XLA Ops:
  9.9 12.9 %convolution_bitcast_fusion = f32[1408,2048]{0,1:T(8,128)} fusion(bf16[1,1152,2048]{2,1,0:T(8,128)(2,1)} %param.15, pred[1152]{0:T(1024)(128)(4,1)S(1)} %iota_compare_fusion, bf16[1,1152,1408]{2,1,0:T(8,128)(2,1)S(1)} %copy-done), kind=kOutput, calls=%fused_computation.3 | convolution fusion | flops 6646136832 | bytes 19498112 | tf_op jit(solution)/shard_map/dot_general | solution.py:74
  22.8 12.0 %copy.42 = f32[1408,2048]{1,0:T(8,128)} copy(f32[1408,2048]{0,1:T(8,128)} %convolution_bitcast_fusion) | data formatting | bytes 23068672
  37.8 2.3 copy.32
  40.1 3.6 copy.33
  43.8 2.4 copy.34
  46.2 105.0 %reduce-scatter.4.cloned.1.call-done = f32[352,2048]{1,0:T(8,128)} async-done(((f32[1408,2048]{1,0:T(8,128)}), f32[352,2048]{1,0:T(8,128)}) %reduce-scatter.4.cloned.1.call-update) | async-done | bytes 2883600
  151.1 2.3 copy.43
  154.9 58.7 %all-reduce.2.cloned.1.call-done = f32[64,2048]{1,0:T(8,128)} async-done(((f32[64,2048]{1,0:T(8,128)}), f32[64,2048]{1,0:T(8,128)}) %all-reduce.2.cloned.1.call-update) | async-done | bytes 524304 | tf_op jit(solution)/shard_map/psum | solution.py:81
  215.4 39.5 %psum.14 = f32[]{:T(128)} all-reduce(f32[]{:T(128)} %multiply_reduce_fusion), channel_id=1, replica_groups=mesh['dp'=4,'expert'=8] {'dp','expert'}, use_global_device_ids=true, to_apply=%region_2.3 | all-reduce | flops 1 | bytes 8 | tf_op jit(solution)/shard_map/psum | solution.py:81
  256.2 6.9 bitcast_subtract_fusion
  263.1 3.4 copy.35
  266.6 4.7 all-to-all-start
  273.5 63.6 %all-to-all-done = f32[352,8,256]{2,0,1:T(8,128)} async-done(((f32[352,8,256]{2,0,1:T(8,128)}), f32[352,8,256]{2,0,1:T(8,128)}, u32[]{:S(2)}, u32[]{:S(2)}) %all-to-all-start) | async-done | bytes 2883616 | tf_op jit(solution)/shard_map/all_to_all | solution.py:39
  337.1 4.4 all-to-all-start.2
  343.9 63.6 %all-to-all-done.2 = f32[352,8,256]{2,0,1:T(8,128)} async-done(((f32[352,8,256]{2,0,1:T(8,128)}), f32[352,8,256]{2,0,1:T(8,128)}, u32[]{:S(2)}, u32[]{:S(2)}) %all-to-all-start.2) | async-done | bytes 2883616 | tf_op jit(solution)/shard_map/all_to_all | solution.py:40
  407.5 4.6 all-to-all-start.4
  412.1 2.5 gather_fusion
  414.7 4.1 gather_fusion.1
  418.8 59.0 %all-to-all-done.4 = f32[352,8,256]{2,0,1:T(8,128)} async-done(((f32[352,8,256]{2,0,1:T(8,128)}), f32[352,8,256]{2,0,1:T(8,128)}, u32[]{:S(2)}, u32[]{:S(2)}) %all-to-all-start.4) | async-done | bytes 2883616 | tf_op jit(solution)/shard_map/all_to_all | solution.py:41
  477.8 4.1 gather_fusion.2
  481.9 6.0 select_bitcast_fusion
  487.9 68.3 %all_to_all.30 = f32[352,8,256]{2,0,1:T(8,128)S(1)} all-to-all(f32[352,8,256]{2,0,1:T(8,128)S(1)} %get-tuple-element.16), channel_id=1, replica_groups=mesh['dp'=4,'expert'=8] {'expert'}, dimensions={1} | all-to-all | bytes 5767168 | tf_op jit(solution)/shard_map/all_to_all | solution.py:35
  556.3 4.4 all-to-all-start.3
  562.2 64.4 %all-to-all-done.3 = f32[352,8,256]{2,0,1:T(8,128)} async-done(((f32[352,8,256]{2,0,1:T(8,128)}), f32[352,8,256]{2,0,1:T(8,128)}, u32[]{:S(2)}, u32[]{:S(2)}) %all-to-all-start.3) | async-done | bytes 2883616 | tf_op jit(solution)/shard_map/all_to_all | solution.py:35
  626.6 4.5 all-to-all-start.5
  631.1 2.9 multiply_subtract_fusion
  634.0 3.2 copy.37
  637.2 4.2 broadcast_in_dim_reshape.9
  641.4 3.5 copy.39
  646.7 50.3 %all-to-all-done.5 = f32[352,8,256]{2,0,1:T(8,128)} async-done(((f32[352,8,256]{2,0,1:T(8,128)}), f32[352,8,256]{2,0,1:T(8,128)}, u32[]{:S(2)}, u32[]{:S(2)}) %all-to-all-start.5) | async-done | bytes 2883616 | tf_op jit(solution)/shard_map/all_to_all | solution.py:35
  696.9 3.5 copy.41
  702.2 6.3 copy.48
  (36 shorter events, 16.9 us)
Async XLA Ops:
  8.0 1.9 copy-start
  8.0 143.1 %reduce-scatter.4.cloned.1.call-start = ((), (), s32[]{:S(2)}) async-start(), calls=%async_computation.9 | async-start | bytes 14417920
  34.8 0.7 copy-start.6
  34.8 3.0 copy-start.4
  34.8 178.7 %all-reduce.2.cloned.1.call-start = ((), (), s32[]{:S(2)}) async-start(), calls=%async_computation.7 | async-start | bytes 1048576 | tf_op jit(solution)/shard_map/psum | solution.py:81
  40.1 3.6 copy-start.5
  266.6 4.7 copy-start.3
  266.6 70.6 %all-to-all-start = ((f32[352,8,256]{2,0,1:T(8,128)}), f32[352,8,256]{2,0,1:T(8,128)}, u32[]{:S(2)}, u32[]{:S(2)}) async-start(f32[352,8,256]{2,0,1:T(8,128)} %copy.35), calls=%async_computation | async-start | bytes 5767168 | tf_op jit(solution)/shard_map/all_to_all | solution.py:39
  273.5 68.1 %copy-start.2 = (f32[352,2048]{0,1:T(8,128)S(1)}, f32[352,2048]{0,1:T(8,128)}, u32[]{:S(2)}) copy-start(f32[352,2048]{0,1:T(8,128)} %get-tuple-element.13) | copy-start | bytes 8650756
  337.1 70.3 %all-to-all-start.2 = ((f32[352,8,256]{2,0,1:T(8,128)}), f32[352,8,256]{2,0,1:T(8,128)}, u32[]{:S(2)}, u32[]{:S(2)}) async-start(f32[352,8,256]{2,0,1:T(8,128)} %copy.38), calls=%async_computation.2 | async-start | bytes 5767168 | tf_op jit(solution)/shard_map/all_to_all | solution.py:40
  343.9 68.2 %copy-start.7 = (s32[8]{0:T(128)S(1)}, s32[8]{0:T(128)}, u32[]{:S(2)}) copy-start(s32[8]{0:T(128)} %param.25) | copy-start | bytes 100
  407.5 70.3 %all-to-all-start.4 = ((f32[352,8,256]{2,0,1:T(8,128)}), f32[352,8,256]{2,0,1:T(8,128)}, u32[]{:S(2)}, u32[]{:S(2)}) async-start(f32[352,8,256]{2,0,1:T(8,128)} %copy.40), calls=%async_computation.4 | async-start | bytes 5767168 | tf_op jit(solution)/shard_map/all_to_all | solution.py:41
  556.3 70.3 %all-to-all-start.3 = ((f32[352,8,256]{2,0,1:T(8,128)}), f32[352,8,256]{2,0,1:T(8,128)}, u32[]{:S(2)}, u32[]{:S(2)}) async-start(f32[352,8,256]{2,0,1:T(8,128)} %get-tuple-element.15), calls=%async_computation.3 | async-start | bytes 5767168 | tf_op jit(solution)/shard_map/all_to_all | solution.py:35
  560.7 141.6 %all-gather.2.cloned.1.call-start = ((), (), s32[]{:S(2)}) async-start(), calls=%async_computation.8 | async-start | bytes 7208960 | tf_op jit(solution)/shard_map/all_gather | solution.py:48
  626.6 70.4 %all-to-all-start.5 = ((f32[352,8,256]{2,0,1:T(8,128)}), f32[352,8,256]{2,0,1:T(8,128)}, u32[]{:S(2)}, u32[]{:S(2)}) async-start(f32[352,8,256]{2,0,1:T(8,128)} %get-tuple-element.14), calls=%async_computation.5 | async-start | bytes 5767168 | tf_op jit(solution)/shard_map/all_to_all | solution.py:35
  702.2 6.3 copy-start.1
Sparse Core Ops, SparseCore 0:
  35.0 116.1 reduce-scatter.3
  563.9 67.7 all-gather.1
Sparse Core Ops, SparseCore 1:
  41.2 172.3 all-reduce.1
where the time goes:
time: 717 us; the launch traced here: 716 us
  waiting for transfers between devices  465 us (65%)
  blocking collectives  108 us (15%)
  local copies, waits for them, and re-layouts  68.8 us (10%)
  starting transfers between devices  22.7 us (3%)
  other arithmetic  19.2 us (3%)
  between operations  17.8 us (2%)
  matrix products  15.1 us (2%)
    all_to_all x2, waiting for transfers between devices, reorder(): lax.all_to_all(arranged, 'expert', split_axis=1, concat_axis=1, tiled=True)  115 us
    unnamed x4, waiting for transfers between devices  105 us
    all_to_all x1, blocking collectives, reorder(): lax.all_to_all(arranged, 'expert', split_axis=1, concat_axis=1, tiled=True)  68.3 us
    all_to_all x1, waiting for transfers between devices, relocate_state(): lax.all_to_all(pieces[1], 'expert', split_axis=1, concat_axis=1, tiled=True)  63.6 us
    all_to_all x1, waiting for transfers between devices, relocate_state(): lax.all_to_all(pieces[0], 'expert', split_axis=1, concat_axis=1, tiled=True)  63.6 us
    all_to_all x1, waiting for transfers between devices, relocate_state(): lax.all_to_all(pieces[2], 'expert', split_axis=1, concat_axis=1, tiled=True)  59 us
    psum x1, waiting for transfers between devices, on_device(): lax.psum((router_partial, jnp.sum(gradient * gradient)), ('dp', 'expert'))  58.7 us
    psum x1, blocking collectives, on_device(): lax.psum((router_partial, jnp.sum(gradient * gradient)), ('dp', 'expert'))  39.5 us
  transfers between devices with their start and end apart: 8, of which 7 were waited for; matrix products, arithmetic and copies ran while one was open for 7% of the time, Pallas kernels for 0%

commit v1 on v0

--- a/solution.py
+++ b/solution.py
@@ -12,6 +12,12 @@
 norm_eps = 1e-06
 correct_first = 1.0 - 0.9**10
 correct_second = 1.0 - 0.95**10
+
+
+def point_the_sectors(in_array):
+    for rr in ("expert", "dp"):
+        in_array = lax.psum(in_array, rr)
+    return in_array
 
 
 def adam_update(gradient, moment_one, moment_two, weights):
@@ -78,9 +84,7 @@
         scatter_dimension=0,
         tiled=True,
     )
-    router_grad, expert_square = lax.psum(
-        (router_partial, jnp.sum(gradient * gradient)), ("dp", "expert")
-    )
+    router_grad, expert_square = point_the_sectors((router_partial, jnp.sum(gradient * gradient)))
     total_square = expert_square + jnp.sum(router_grad * router_grad)
     clip_limit = 2.0 * math.sqrt(
         float(lax.axis_size("expert") * hidden_units * features + router_cot.shape[0] * features)

time: 717 us -> 673 us (0.939)
  waiting for transfers between devices: 465 us -> 433 us
  blocking collectives: 108 us -> 94.6 us
    unnamed x4 -> x5, waiting for transfers between devices: 105 us -> 73.8 us
    psum x1 -> x2, blocking collectives: 39.5 us -> 26.3 us  [point_the_sectors(): in_array = lax.psum(in_array, rr)]
    unnamed x22 -> x18, local copies, waits for them, and re-layouts: 30.8 us -> 30 us
    psum x1 -> x2, waiting for transfers between devices: 58.7 us -> 58.7 us  [point_the_sectors(): in_array = lax.psum(in_array, rr)]
  transfers between devices with their start and end apart: 8 -> 9, of which waited for: 7 -> 8; matrix products, arithmetic and copies ran while one was open for 7% -> 11% of each run, Pallas kernels for 0% -> 0%
where the time goes in v1:
time: 673 us; the launch traced here: 671 us
  waiting for transfers between devices  433 us (64%)
  blocking collectives  94.6 us (14%)
  local copies, waits for them, and re-layouts  68.1 us (10%)
  starting transfers between devices  23 us (3%)
  other arithmetic  19.2 us (3%)
  between operations  17.8 us (3%)
  matrix products  15.1 us (2%)
    all_to_all x2, waiting for transfers between devices, reorder(): lax.all_to_all(arranged, 'expert', split_axis=1, concat_axis=1, tiled=True)  115 us
    unnamed x5, waiting for transfers between devices  73.8 us
    all_to_all x1, blocking collectives, reorder(): lax.all_to_all(arranged, 'expert', split_axis=1, concat_axis=1, tiled=True)  68.3 us
    all_to_all x1, waiting for transfers between devices, relocate_state(): lax.all_to_all(pieces[0], 'expert', split_axis=1, concat_axis=1, tiled=True)  63.7 us
    all_to_all x1, waiting for transfers between devices, relocate_state(): lax.all_to_all(pieces[1], 'expert', split_axis=1, concat_axis=1, tiled=True)  63.6 us
    all_to_all x1, waiting for transfers between devices, relocate_state(): lax.all_to_all(pieces[2], 'expert', split_axis=1, concat_axis=1, tiled=True)  59 us
    psum x2, waiting for transfers between devices, point_the_sectors(): in_array = lax.psum(in_array, rr)  58.7 us
    unnamed x18, local copies, waits for them, and re-layouts  30 us
  transfers between devices with their start and end apart: 9, of which 8 were waited for; matrix products, arithmetic and copies ran while one was open for 11% of the time, Pallas kernels for 0%

profile of v1, /device:TPU:0, one launch (start us, length us, event | category | flops | bytes accessed | tf_op | source)
XLA Modules:
  0.0 671.3 jit_solution(11135036594333607445)
XLA Ops:
  11.0 12.9 %convolution_bitcast_fusion = f32[1408,2048]{0,1:T(8,128)} fusion(bf16[1,1152,2048]{2,1,0:T(8,128)(2,1)} %param.15, pred[1152]{0:T(1024)(128)(4,1)S(1)} %iota_compare_fusion, bf16[1,1152,1408]{2,1,0:T(8,128)(2,1)S(1)} %copy-done), kind=kOutput, calls=%fused_computation.3 | convolution fusion | flops 6646136832 | bytes 19498112 | tf_op jit(solution)/shard_map/dot_general | solution.py:80
  23.9 12.0 %copy.42 = f32[1408,2048]{1,0:T(8,128)} copy(f32[1408,2048]{0,1:T(8,128)} %convolution_bitcast_fusion) | data formatting | bytes 23068672
  36.0 35.0 %all-reduce.3.cloned.1.call-done = f32[64,2048]{1,0:T(8,128)} async-done(((f32[64,2048]{1,0:T(8,128)}), f32[64,2048]{1,0:T(8,128)}) %all-reduce.3.cloned.1.call-update) | async-done | bytes 524304 | tf_op jit(solution)/shard_map/psum | solution.py:19
  73.4 3.6 copy.33
  76.9 73.8 %reduce-scatter.4.cloned.1.call-done = f32[352,2048]{1,0:T(8,128)} async-done(((f32[1408,2048]{1,0:T(8,128)}), f32[352,2048]{1,0:T(8,128)}) %reduce-scatter.4.cloned.1.call-update) | async-done | bytes 2883600
  154.4 3.5 copy.34
  157.9 16.8 %psum.28 = f32[]{:T(128)} all-reduce(f32[]{:T(128)} %multiply_reduce_fusion), channel_id=1, replica_groups=mesh['dp'=4,'expert'=8] {'expert'}, use_global_device_ids=true, to_apply=%region_2.3 | all-reduce | flops 1 | bytes 8 | tf_op jit(solution)/shard_map/psum | solution.py:19
  174.7 23.7 %all-reduce.5.cloned.1.call-done = f32[64,2048]{1,0:T(8,128)} async-done(((f32[64,2048]{1,0:T(8,128)}), f32[64,2048]{1,0:T(8,128)}) %all-reduce.5.cloned.1.call-update) | async-done | bytes 524304 | tf_op jit(solution)/shard_map/psum | solution.py:19
  200.2 9.5 %psum.29 = f32[]{:T(128)} all-reduce(f32[]{:T(128)} %psum.28), channel_id=1, replica_groups=mesh['dp'=4,'expert'=8] {'dp'}, use_global_device_ids=true, to_apply=%region_3.4 | all-reduce | flops 1 | bytes 8 | tf_op jit(solution)/shard_map/psum | solution.py:19
  211.1 6.9 %bitcast_subtract_fusion = (f32[352,2048]{0,1:T(8,128)}, f32[352,2048]{0,1:T(8,128)}, f32[352,2048]{0,1:T(8,128)}) fusion(f32[1,352,2048]{1,2,0:T(8,128)} %copy.32, f32[352,2048]{0,1:T(8,128)S(1)} %copy.43, f32[]{:T(128)S(6)} %min_shard_map.3, f32[1,352,2048]{1,2,0:T(8,128)} %copy.33, f32[1,352,2048]{1,2,0:T(8,128)} %copy.34), kind=kLoop, calls=%fused_computation.11 | loop fusion | flops 11534336 | bytes 20185092 | tf_op jit(solution)/shard_map/sub | solution.py:27
  218.0 3.4 copy.35
  221.4 4.9 all-to-all-start
  228.6 63.7 %all-to-all-done = f32[352,8,256]{2,0,1:T(8,128)} async-done(((f32[352,8,256]{2,0,1:T(8,128)}), f32[352,8,256]{2,0,1:T(8,128)}, u32[]{:S(2)}, u32[]{:S(2)}) %all-to-all-start) | async-done | bytes 2883616 | tf_op jit(solution)/shard_map/all_to_all | solution.py:45
  292.3 4.4 all-to-all-start.2
  299.0 63.6 %all-to-all-done.2 = f32[352,8,256]{2,0,1:T(8,128)} async-done(((f32[352,8,256]{2,0,1:T(8,128)}), f32[352,8,256]{2,0,1:T(8,128)}, u32[]{:S(2)}, u32[]{:S(2)}) %all-to-all-start.2) | async-done | bytes 2883616 | tf_op jit(solution)/shard_map/all_to_all | solution.py:46
  362.6 4.6 all-to-all-start.4
  367.3 2.5 gather_fusion
  369.8 4.1 gather_fusion.1
  373.9 59.0 %all-to-all-done.4 = f32[352,8,256]{2,0,1:T(8,128)} async-done(((f32[352,8,256]{2,0,1:T(8,128)}), f32[352,8,256]{2,0,1:T(8,128)}, u32[]{:S(2)}, u32[]{:S(2)}) %all-to-all-start.4) | async-done | bytes 2883616 | tf_op jit(solution)/shard_map/all_to_all | solution.py:47
  432.9 4.1 gather_fusion.2
  437.0 6.0 select_bitcast_fusion
  443.1 68.3 %all_to_all.30 = f32[352,8,256]{2,0,1:T(8,128)S(1)} all-to-all(f32[352,8,256]{2,0,1:T(8,128)S(1)} %get-tuple-element.16), channel_id=1, replica_groups=mesh['dp'=4,'expert'=8] {'expert'}, dimensions={1} | all-to-all | bytes 5767168 | tf_op jit(solution)/shard_map/all_to_all | solution.py:41
  511.4 4.4 all-to-all-start.3
  517.4 64.4 %all-to-all-done.3 = f32[352,8,256]{2,0,1:T(8,128)} async-done(((f32[352,8,256]{2,0,1:T(8,128)}), f32[352,8,256]{2,0,1:T(8,128)}, u32[]{:S(2)}, u32[]{:S(2)}) %all-to-all-start.3) | async-done | bytes 2883616 | tf_op jit(solution)/shard_map/all_to_all | solution.py:41
  581.7 4.5 all-to-all-start.5
  586.2 2.9 multiply_subtract_fusion
  589.1 3.2 copy.37
  592.4 4.2 broadcast_in_dim_reshape.9
  596.5 3.5 copy.39
  601.8 50.3 %all-to-all-done.5 = f32[352,8,256]{2,0,1:T(8,128)} async-done(((f32[352,8,256]{2,0,1:T(8,128)}), f32[352,8,256]{2,0,1:T(8,128)}, u32[]{:S(2)}, u32[]{:S(2)}) %all-to-all-start.5) | async-done | bytes 2883616 | tf_op jit(solution)/shard_map/all_to_all | solution.py:41
  652.1 3.5 copy.41
  657.4 6.3 copy.49
  (36 shorter events, 20.0 us)
Async XLA Ops:
  8.0 3.0 copy-start
  8.0 63.0 %all-reduce.3.cloned.1.call-start = ((), (), s32[]{:S(2)}) async-start(), calls=%async_computation.7 | async-start | bytes 1048576 | tf_op jit(solution)/shard_map/psum | solution.py:19
  10.3 140.4 %reduce-scatter.4.cloned.1.call-start = ((), (), s32[]{:S(2)}) async-start(), calls=%async_computation.10 | async-start | bytes 14417920
  35.9 35.1 %copy-start.4 = (f32[1,352,2048]{2,1,0:T(8,128)S(1)}, f32[1,352,2048]{2,1,0:T(8,128)}, u32[]{:S(2)}) copy-start(f32[1,352,2048]{2,1,0:T(8,128)} %param.17) | copy-start | bytes 8650756
  35.9 162.4 %all-reduce.5.cloned.1.call-start = ((), (), s32[]{:S(2)}) async-start(), calls=%async_computation.8 | async-start | bytes 1048576 | tf_op jit(solution)/shard_map/psum | solution.py:19
  221.4 4.9 copy-start.3
  221.4 70.9 %all-to-all-start = ((f32[352,8,256]{2,0,1:T(8,128)}), f32[352,8,256]{2,0,1:T(8,128)}, u32[]{:S(2)}, u32[]{:S(2)}) async-start(f32[352,8,256]{2,0,1:T(8,128)} %copy.35), calls=%async_computation | async-start | bytes 5767168 | tf_op jit(solution)/shard_map/all_to_all | solution.py:45
  228.6 68.2 %copy-start.2 = (f32[352,2048]{0,1:T(8,128)S(1)}, f32[352,2048]{0,1:T(8,128)}, u32[]{:S(2)}) copy-start(f32[352,2048]{0,1:T(8,128)} %get-tuple-element.13) | copy-start | bytes 8650756
  292.3 70.3 %all-to-all-start.2 = ((f32[352,8,256]{2,0,1:T(8,128)}), f32[352,8,256]{2,0,1:T(8,128)}, u32[]{:S(2)}, u32[]{:S(2)}) async-start(f32[352,8,256]{2,0,1:T(8,128)} %copy.38), calls=%async_computation.2 | async-start | bytes 5767168 | tf_op jit(solution)/shard_map/all_to_all | solution.py:46
  299.0 68.2 %copy-start.5 = (s32[8]{0:T(128)S(1)}, s32[8]{0:T(128)}, u32[]{:S(2)}) copy-start(s32[8]{0:T(128)} %param.25) | copy-start | bytes 100
  362.6 70.3 %all-to-all-start.4 = ((f32[352,8,256]{2,0,1:T(8,128)}), f32[352,8,256]{2,0,1:T(8,128)}, u32[]{:S(2)}, u32[]{:S(2)}) async-start(f32[352,8,256]{2,0,1:T(8,128)} %copy.40), calls=%async_computation.4 | async-start | bytes 5767168 | tf_op jit(solution)/shard_map/all_to_all | solution.py:47
  511.4 70.3 %all-to-all-start.3 = ((f32[352,8,256]{2,0,1:T(8,128)}), f32[352,8,256]{2,0,1:T(8,128)}, u32[]{:S(2)}, u32[]{:S(2)}) async-start(f32[352,8,256]{2,0,1:T(8,128)} %get-tuple-element.15), calls=%async_computation.3 | async-start | bytes 5767168 | tf_op jit(solution)/shard_map/all_to_all | solution.py:41
  515.9 141.5 %all-gather.2.cloned.1.call-start = ((), (), s32[]{:S(2)}) async-start(), calls=%async_computation.9 | async-start | bytes 7208960 | tf_op jit(solution)/shard_map/all_gather | solution.py:54
  581.7 70.4 %all-to-all-start.5 = ((f32[352,8,256]{2,0,1:T(8,128)}), f32[352,8,256]{2,0,1:T(8,128)}, u32[]{:S(2)}, u32[]{:S(2)}) async-start(f32[352,8,256]{2,0,1:T(8,128)} %get-tuple-element.14), calls=%async_computation.5 | async-start | bytes 5767168 | tf_op jit(solution)/shard_map/all_to_all | solution.py:41
  657.4 6.3 copy-start.1
Sparse Core Ops, SparseCore 0:
  11.7 59.2 all-reduce.2
Sparse Core Ops, SparseCore 1:
  36.0 114.6 reduce-scatter.3
  153.6 44.8 all-reduce.4
  518.8 65.9 all-gather.1
